TPU v7x, 512 devices: a whole 4x8x8 slice. The times are simulated.
512 devices in a mesh: lag: 16 (over y_lo, z), elem: 32 (over y_hi, x, core).
Axes of the slice: x: 4, y: 8 (y_hi: 4, y_lo: 2; y = y_hi * 2 + y_lo), z: 8, core: 2. Of those that a mesh axis runs over, the one named last changes fastest.
Arguments:
- kernel_tiles: bfloat16 [16, 32768, 1536], P('lag', 'elem'), may hold values from -0.0390625 to 0.0390625
- shell_index: int32 [16, 32, 3], P('lag', 'elem'), may hold values from 0 to 5
- cone_blocks: int32 [16], P('lag'), may hold values from 1 to 3
- history: bfloat16 [16, 32768, 256], P('lag', 'elem'), may hold values from -6 to 6
- prestress: float32 [32, 16, 64, 256], P('elem', 'lag'), may hold values from -6 to 6
- log_state: float32 [32, 16, 64, 256], P('elem', 'lag'), may hold values from -0.7 to 0.7
- fric_a: float32 [32, 16, 64], P('elem', 'lag'), may hold values from 0.3 to 1
- fric_b: float32 [32, 16, 64], P('elem', 'lag'), may hold values from 0.3 to 1
- normal_stress: float32 [32, 16, 64], P('elem', 'lag'), may hold values from 1 to 4
Outputs:
- final_rates: bfloat16 [32, 16, 64, 256], P('elem', 'lag')
- final_state: float32 [32, 16, 64, 256], P('elem', 'lag')
Inputs may be any that keep to these rules, and one draw needn't show every extreme that they name: `shell_index`: 0 and 1 name the two blocks of the element block below the receiver block, 2 and 3 its own, 4 and 5 those of the block above.
All inputs are finite; a program needn't handle non-finite values.
Results may differ from a plain program's by a relative error of at most 0.0034.
Values may be sent and summed in bfloat16 or wider, within the bound.
A program may use at most 64 MiB of HBM per device.

v0:
```python
import jax
import jax.numpy as jnp
from jax import lax
from jax.sharding import PartitionSpec as P

BLOCK = 512
SHELL = 3
STEPS = 4
NEWTON = 3


damping = 0.5
time_step = 0.25
creep_square = 0.01


def padded(value, sides, width):
    for axis, dim in sides:
        count, length = (lax.axis_size(axis), value.shape[dim])
        up = [(i, (i + 1) % count) for i in range(count - 1)]
        down = [(j, i) for i, j in up]
        last = lax.slice_in_dim(value, length - width, length, axis=dim)
        leading = lax.slice_in_dim(value, 0, width, axis=dim)
        before = lax.ppermute(last, axis, up)
        after = lax.ppermute(leading, axis, down)
        value = jnp.concatenate([before, value, after], axis=dim)
    return value


def cut_along(value, dim, count):
    lengths = value.shape
    blocks = value.reshape(*lengths[:dim], count, lengths[dim] // count, *lengths[dim + 1 :])
    return jnp.moveaxis(blocks, dim, 0)


def summed_on_arrival(value, axis, dim):
    blocks = cut_along(value, dim, lax.axis_size(axis))
    arrived = lax.all_to_all(blocks, axis, split_axis=0, concat_axis=0, tiled=True)
    return arrived.sum(axis=0)


def joined_along(blocks, dim):
    lengths = list(blocks.shape[1:])
    lengths[dim] *= blocks.shape[0]
    return jnp.moveaxis(blocks, 0, dim).reshape(lengths)


def from_everyone(value, axis):
    copies = jnp.broadcast_to(value, (lax.axis_size(axis), *value.shape))
    return lax.all_to_all(copies, axis, split_axis=0, concat_axis=0, tiled=True)


def gather_directly(value, axis, dim):
    return joined_along(from_everyone(value, axis), dim)


def passed_along(block, axis, distance):
    devices = range(lax.axis_size(axis))
    route = [(i - distance, i) for i in devices if i - distance in devices]
    return lax.ppermute(block, axis, route)


def inverse_sinh(value):
    magnitude = jnp.abs(value)
    positive = jnp.log(magnitude + jnp.sqrt(magnitude * magnitude + 1.0))
    return jnp.where(value < 0.0, -positive, positive)


def pick_sources(window, shell_pick, live_count):
    pieces = []
    for shell_slot in range(SHELL):
        row_start = shell_pick[shell_slot] * BLOCK
        source_block = lax.dynamic_slice_in_dim(window, row_start, BLOCK, 0)
        pieces.append(jnp.where(shell_slot < live_count, source_block, jnp.zeros((), jnp.bfloat16)))
    return jnp.concatenate(pieces, 0)


def settle_friction(shear_load, state_now, coef_a, coef_b, sigma):
    scale = 0.5 * jnp.exp(coef_b / coef_a * state_now)
    strength = sigma * coef_a
    velocity = shear_load / (strength * scale + damping)
    for iteration in range(NEWTON):
        scaled = scale * velocity
        residual = strength * inverse_sinh(scaled) + damping * velocity - shear_load
        derivative = strength * scale / jnp.sqrt(1.0 + scaled * scaled) + damping
        velocity = velocity - residual / derivative
    speed = jnp.sqrt(velocity * velocity + creep_square)
    new_state = state_now + time_step * (jnp.exp(-state_now) - speed)
    return (velocity.astype(jnp.bfloat16), new_state)


def shards(
    kernel_tiles,
    shell_index,
    cone_blocks,
    history,
    prestress,
    log_state,
    fric_a,
    fric_b,
    normal_stress,
):
    kernel_tile = kernel_tiles[0]
    lag_rates = history[0]
    shell_pick = shell_index[0, 0]
    live_count = cone_blocks[0]
    first_lag = lax.axis_index("lag") == 0
    own_rows = prestress.shape[2]
    scenarios = prestress.shape[3]
    stress_rows = prestress[0, 0]
    state_rows = log_state[0, 0]
    coef_a = fric_a[0, 0][:, None]
    coef_b = fric_b[0, 0][:, None]
    sigma = normal_stress[0, 0][:, None]
    new_rates = lag_rates
    for step_index in range(STEPS):
        window = padded(lag_rates, (("elem", 0),), lag_rates.shape[0])
        sources = pick_sources(window, shell_pick, live_count)
        traction = summed_on_arrival(
            jnp.dot(kernel_tile, sources, preferred_element_type=jnp.float32), "lag", 0
        )
        new_rates, state_rows = settle_friction(
            stress_rows + traction, state_rows, coef_a, coef_b, sigma
        )
        if step_index + 1 < STEPS:
            arrived = gather_directly(new_rates, "lag", 0)
        if step_index + 1 < STEPS:
            older = passed_along(lag_rates, "lag", 1)
            lag_rates = jnp.where(first_lag, arrived, older)
    return (
        new_rates.reshape(1, 1, own_rows, scenarios),
        state_rows.reshape(1, 1, own_rows, scenarios),
    )


def solution(mesh):
    in_specs = (
        P("lag", "elem", None),
        P("lag", "elem", None),
        P("lag"),
        P("lag", "elem", None),
        P("elem", "lag", None, None),
        P("elem", "lag", None, None),
        P("elem", "lag", None),
        P("elem", "lag", None),
        P("elem", "lag", None),
    )
    out_specs = (P("elem", "lag", None, None), P("elem", "lag", None, None))
    return jax.shard_map(shards, mesh=mesh, in_specs=in_specs, out_specs=out_specs, check_vma=False)
```

profile of v0, /device:TPU:47, one launch (start us, length us, event | category | flops | bytes accessed | tf_op | source)
XLA Modules:
  0.0 323.3 jit_solution(1261200651825524661)
XLA Ops:
  0.6 0.0 copy-start
  0.6 3.2 collective-permute-start
  3.8 1.9 collective-permute-start.1
  5.7 1.4 fusion.162
  9.7 6.2 %collective-permute-done = bf16[1024,256]{1,0:T(8,128)(2,1)} collective-permute-done((bf16[1024,256]{1,0:T(8,128)(2,1)}, bf16[1024,256]{1,0:T(8,128)(2,1)}, u32[]{:S(2)}, u32[]{:S(2)}) %collective-permute-start) | collective-permute-done | bytes 524320 | tf_op jit(solution)/shard_map/ppermute | solution.py:24
  15.9 1.9 collective-permute-done.1
  17.7 1.5 pad_maximum_fusion
  19.2 0.2 dynamic-slice_select_fusion.11
  19.4 2.0 fusion.8
  21.4 2.6 copy.11
  23.9 0.0 copy-start.6
  24.0 16.9 %all-to-all-start = ((f32[16,64,256]{2,1,0:T(8,128)}), f32[16,64,256]{2,1,0:T(8,128)}, u32[]{:S(2)}, u32[]{:S(2)}) async-start(f32[16,64,256]{2,1,0:T(8,128)} %bitcast.100), calls=%async_computation | async-start | bytes 2097152 | tf_op jit(solution)/shard_map/all_to_all | solution.py:38
  40.9 17.6 %all-to-all-done = f32[16,64,256]{2,1,0:T(8,128)} async-done(((f32[16,64,256]{2,1,0:T(8,128)}), f32[16,64,256]{2,1,0:T(8,128)}, u32[]{:S(2)}, u32[]{:S(2)}) %all-to-all-start) | async-done | bytes 1048608 | tf_op jit(solution)/shard_map/all_to_all | solution.py:38
  58.5 1.3 reduce_sum.44
  59.8 0.3 fusion.160
  60.1 0.8 broadcast_in_dim.25
  60.9 6.9 %all-to-all-start.1 = ((bf16[16,64,256]{2,1,0:T(8,128)(2,1)}), bf16[16,64,256]{2,1,0:T(8,128)(2,1)}, u32[]{:S(2)}, u32[]{:S(2)}) async-start(bf16[16,64,256]{2,1,0:T(8,128)(2,1)} %broadcast_in_dim.25), calls=%async_computation.1 | async-start | bytes 1048576 | tf_op jit(solution)/shard_map/all_to_all | solution.py:50
  67.8 3.1 collective-permute-start.2
  70.9 21.0 %collective-permute-done.2 = bf16[1024,256]{1,0:T(8,128)(2,1)} collective-permute-done((bf16[1024,256]{1,0:T(8,128)(2,1)}, bf16[1024,256]{1,0:T(8,128)(2,1)}, u32[]{:S(2)}, u32[]{:S(2)}) %collective-permute-start.2) | collective-permute-done | bytes 524320 | tf_op jit(solution)/shard_map/ppermute | solution.py:60
  91.9 1.3 bitcast_select_fusion.2
  93.2 5.3 %collective-permute-start.3 = (bf16[1024,256]{1,0:T(8,128)(2,1)S(1)}, bf16[1024,256]{1,0:T(8,128)(2,1)S(1)}, u32[]{:S(2)}, u32[]{:S(2)}) collective-permute-start(bf16[1024,256]{1,0:T(8,128)(2,1)S(1)} %bitcast_select_fusion.2), channel_id=1, source_target_pairs={{0,1},{1,2},{2,3},{3,4},{4,5},{5,6},{6,7},{7,8},{8,9},{9,10},{10,1... | collective-permute-start | bytes 1572872 | tf_op jit(solution)/shard_map/ppermute | solution.py:24
  98.5 1.9 collective-permute-start.4
  100.4 6.6 %collective-permute-done.3 = bf16[1024,256]{1,0:T(8,128)(2,1)S(1)} collective-permute-done((bf16[1024,256]{1,0:T(8,128)(2,1)S(1)}, bf16[1024,256]{1,0:T(8,128)(2,1)S(1)}, u32[]{:S(2)}, u32[]{:S(2)}) %collective-permute-start.3) | collective-permute-done | bytes 524320 | tf_op jit(solution)/shard_map/ppermute | solution.py:24
  107.0 5.1 %collective-permute-done.4 = bf16[1024,256]{1,0:T(8,128)(2,1)S(1)} collective-permute-done((bf16[1024,256]{1,0:T(8,128)(2,1)S(1)}, bf16[1024,256]{1,0:T(8,128)(2,1)S(1)}, u32[]{:S(2)}, u32[]{:S(2)}) %collective-permute-start.4) | collective-permute-done | bytes 524320 | tf_op jit(solution)/shard_map/ppermute | solution.py:25
  112.1 0.1 pad_maximum_fusion.1
  112.2 0.2 dynamic-slice_select_fusion.8
  112.4 2.0 fusion.11
  114.4 2.6 copy.12
  116.9 29.7 %all_to_all.35 = f32[16,64,256]{2,1,0:T(8,128)} all-to-all(f32[16,64,256]{2,1,0:T(8,128)} %bitcast.101), channel_id=1, replica_groups=mesh['lag'=16,'elem'=32] {'lag'}, dimensions={0} | all-to-all | bytes 2097152 | tf_op jit(solution)/shard_map/all_to_all | solution.py:38
  146.6 1.3 reduce_sum.45
  147.9 0.9 fusion.158
  148.9 0.8 broadcast_in_dim.26
  149.7 4.4 %all-to-all-start.3 = ((bf16[16,64,256]{2,1,0:T(8,128)(2,1)}), bf16[16,64,256]{2,1,0:T(8,128)(2,1)}, u32[]{:S(2)}, u32[]{:S(2)}) async-start(bf16[16,64,256]{2,1,0:T(8,128)(2,1)} %broadcast_in_dim.26), calls=%async_computation.3 | async-start | bytes 1048576 | tf_op jit(solution)/shard_map/all_to_all | solution.py:50
  154.1 3.1 collective-permute-start.5
  157.1 21.6 %collective-permute-done.5 = bf16[1024,256]{1,0:T(8,128)(2,1)} collective-permute-done((bf16[1024,256]{1,0:T(8,128)(2,1)}, bf16[1024,256]{1,0:T(8,128)(2,1)}, u32[]{:S(2)}, u32[]{:S(2)}) %collective-permute-start.5) | collective-permute-done | bytes 524320 | tf_op jit(solution)/shard_map/ppermute | solution.py:60
  178.7 1.3 bitcast_select_fusion.1
  180.0 5.2 %collective-permute-start.6 = (bf16[1024,256]{1,0:T(8,128)(2,1)S(1)}, bf16[1024,256]{1,0:T(8,128)(2,1)S(1)}, u32[]{:S(2)}, u32[]{:S(2)}) collective-permute-start(bf16[1024,256]{1,0:T(8,128)(2,1)S(1)} %bitcast_select_fusion.1), channel_id=1, source_target_pairs={{0,1},{1,2},{2,3},{3,4},{4,5},{5,6},{6,7},{7,8},{8,9},{9,10},{10,1... | collective-permute-start | bytes 1572872 | tf_op jit(solution)/shard_map/ppermute | solution.py:24
  185.2 1.9 collective-permute-start.7
  187.1 6.6 %collective-permute-done.6 = bf16[1024,256]{1,0:T(8,128)(2,1)S(1)} collective-permute-done((bf16[1024,256]{1,0:T(8,128)(2,1)S(1)}, bf16[1024,256]{1,0:T(8,128)(2,1)S(1)}, u32[]{:S(2)}, u32[]{:S(2)}) %collective-permute-start.6) | collective-permute-done | bytes 524320 | tf_op jit(solution)/shard_map/ppermute | solution.py:24
  193.7 5.1 %collective-permute-done.7 = bf16[1024,256]{1,0:T(8,128)(2,1)S(1)} collective-permute-done((bf16[1024,256]{1,0:T(8,128)(2,1)S(1)}, bf16[1024,256]{1,0:T(8,128)(2,1)S(1)}, u32[]{:S(2)}, u32[]{:S(2)}) %collective-permute-start.7) | collective-permute-done | bytes 524320 | tf_op jit(solution)/shard_map/ppermute | solution.py:25
  198.8 0.1 pad_maximum_fusion.2
  198.9 0.2 dynamic-slice_select_fusion.5
  199.1 2.0 fusion.14
  201.1 2.6 copy.13
  203.6 28.8 %all_to_all.36 = f32[16,64,256]{2,1,0:T(8,128)} all-to-all(f32[16,64,256]{2,1,0:T(8,128)} %bitcast.102), channel_id=1, replica_groups=mesh['lag'=16,'elem'=32] {'lag'}, dimensions={0} | all-to-all | bytes 2097152 | tf_op jit(solution)/shard_map/all_to_all | solution.py:38
  232.5 1.3 reduce_sum.46
  233.7 1.1 fusion.152
  234.9 0.8 broadcast_in_dim.27
  235.7 4.7 %all-to-all-start.5 = ((bf16[16,64,256]{2,1,0:T(8,128)(2,1)}), bf16[16,64,256]{2,1,0:T(8,128)(2,1)}, u32[]{:S(2)}, u32[]{:S(2)}) async-start(bf16[16,64,256]{2,1,0:T(8,128)(2,1)} %broadcast_in_dim.27), calls=%async_computation.5 | async-start | bytes 1048576 | tf_op jit(solution)/shard_map/all_to_all | solution.py:50
  240.4 3.1 collective-permute-start.8
  243.5 21.4 %collective-permute-done.8 = bf16[1024,256]{1,0:T(8,128)(2,1)} collective-permute-done((bf16[1024,256]{1,0:T(8,128)(2,1)}, bf16[1024,256]{1,0:T(8,128)(2,1)}, u32[]{:S(2)}, u32[]{:S(2)}) %collective-permute-start.8) | collective-permute-done | bytes 524320 | tf_op jit(solution)/shard_map/ppermute | solution.py:60
  265.0 0.8 all-to-all-done.5
  265.7 1.3 bitcast_select_fusion
  267.0 1.9 collective-permute-start.10
  268.9 6.7 %collective-permute-start.9 = (bf16[1024,256]{1,0:T(8,128)(2,1)S(1)}, bf16[1024,256]{1,0:T(8,128)(2,1)S(1)}, u32[]{:S(2)}, u32[]{:S(2)}) collective-permute-start(bf16[1024,256]{1,0:T(8,128)(2,1)S(1)} %bitcast_select_fusion), channel_id=1, source_target_pairs={{0,1},{1,2},{2,3},{3,4},{4,5},{5,6},{6,7},{7,8},{8,9},{9,10},{10,1... | collective-permute-start | bytes 1572872 | tf_op jit(solution)/shard_map/ppermute | solution.py:24
  275.6 5.0 %collective-permute-done.10 = bf16[1024,256]{1,0:T(8,128)(2,1)S(1)} collective-permute-done((bf16[1024,256]{1,0:T(8,128)(2,1)S(1)}, bf16[1024,256]{1,0:T(8,128)(2,1)S(1)}, u32[]{:S(2)}, u32[]{:S(2)}) %collective-permute-start.10) | collective-permute-done | bytes 524320 | tf_op jit(solution)/shard_map/ppermute | solution.py:25
  280.6 3.5 %collective-permute-done.9 = bf16[1024,256]{1,0:T(8,128)(2,1)S(1)} collective-permute-done((bf16[1024,256]{1,0:T(8,128)(2,1)S(1)}, bf16[1024,256]{1,0:T(8,128)(2,1)S(1)}, u32[]{:S(2)}, u32[]{:S(2)}) %collective-permute-start.9) | collective-permute-done | bytes 524320 | tf_op jit(solution)/shard_map/ppermute | solution.py:24
  284.1 0.1 pad_maximum_fusion.3
  284.2 0.2 dynamic-slice_select_fusion.2
  284.4 2.0 fusion.17
  286.4 2.6 copy.14
  288.9 31.2 %all_to_all.37 = f32[16,64,256]{2,1,0:T(8,128)} all-to-all(f32[16,64,256]{2,1,0:T(8,128)} %bitcast.103), channel_id=1, replica_groups=mesh['lag'=16,'elem'=32] {'lag'}, dimensions={0} | all-to-all | bytes 2097152 | tf_op jit(solution)/shard_map/all_to_all | solution.py:38
  320.2 1.3 reduce_sum.47
  321.5 1.8 multiply_add_fusion
  (18 shorter events, 0.0 us)
Async XLA Ops:
  0.6 18.7 %copy-start = (bf16[1,1024,1536]{2,1,0:T(8,128)(2,1)S(1)}, bf16[1,1024,1536]{2,1,0:T(8,128)(2,1)}, u32[]{:S(2)}) copy-start(bf16[1,1024,1536]{2,1,0:T(8,128)(2,1)} %param.9) | copy-start | bytes 9437188
  0.6 15.2 %collective-permute-start = (bf16[1024,256]{1,0:T(8,128)(2,1)}, bf16[1024,256]{1,0:T(8,128)(2,1)}, u32[]{:S(2)}, u32[]{:S(2)}) collective-permute-start(bf16[1024,256]{1,0:T(8,128)(2,1)} %bitcast.104), channel_id=1, source_target_pairs={{0,1},{1,2},{2,3},{3,4},{4,5},{5,6},{6,7},{7,8},{8,9},{9,10},{10,1... | collective-permute-start | bytes 1572872 | tf_op jit(solution)/shard_map/ppermute | solution.py:24
  3.8 13.9 %collective-permute-start.1 = (bf16[1024,256]{1,0:T(8,128)(2,1)}, bf16[1024,256]{1,0:T(8,128)(2,1)}, u32[]{:S(2)}, u32[]{:S(2)}) collective-permute-start(bf16[1024,256]{1,0:T(8,128)(2,1)} %bitcast.105), channel_id=1, source_target_pairs={{1,0},{2,1},{3,2},{4,3},{5,4},{6,5},{7,6},{8,7},{9,8},{10,9},{11,1... | collective-permute-start | bytes 1572872 | tf_op jit(solution)/shard_map/ppermute | solution.py:25
  23.9 16.9 %copy-start.4 = (f32[1,1,64]{2,1,0:T(1,128)S(1)}, f32[1,1,64]{2,1,0:T(1,128)}, u32[]{:S(2)}) copy-start(f32[1,1,64]{2,1,0:T(1,128)} %param.15) | copy-start | bytes 772
  23.9 16.9 %copy-start.7 = (f32[1,1,64]{2,1,0:T(1,128)S(1)}, f32[1,1,64]{2,1,0:T(1,128)}, u32[]{:S(2)}) copy-start(f32[1,1,64]{2,1,0:T(1,128)} %param.16) | copy-start | bytes 772
  23.9 16.9 %copy-start.3 = (f32[1,1,64]{2,1,0:T(1,128)S(1)}, f32[1,1,64]{2,1,0:T(1,128)}, u32[]{:S(2)}) copy-start(f32[1,1,64]{2,1,0:T(1,128)} %param.17) | copy-start | bytes 772
  23.9 35.8 %copy-start.5 = (f32[1,1,64,256]{3,2,1,0:T(8,128)S(1)}, f32[1,1,64,256]{3,2,1,0:T(8,128)}, u32[]{:S(2)}) copy-start(f32[1,1,64,256]{3,2,1,0:T(8,128)} %param.13) | copy-start | bytes 196612
  23.9 35.8 %copy-start.6 = (f32[1,1,64,256]{3,2,1,0:T(8,128)S(1)}, f32[1,1,64,256]{3,2,1,0:T(8,128)}, u32[]{:S(2)}) copy-start(f32[1,1,64,256]{3,2,1,0:T(8,128)} %param.14) | copy-start | bytes 196612
  24.0 34.5 %all-to-all-start = ((f32[16,64,256]{2,1,0:T(8,128)}), f32[16,64,256]{2,1,0:T(8,128)}, u32[]{:S(2)}, u32[]{:S(2)}) async-start(f32[16,64,256]{2,1,0:T(8,128)} %bitcast.100), calls=%async_computation | async-start | bytes 2097152 | tf_op jit(solution)/shard_map/all_to_all | solution.py:38
  60.9 31.0 %all-to-all-start.1 = ((bf16[16,64,256]{2,1,0:T(8,128)(2,1)}), bf16[16,64,256]{2,1,0:T(8,128)(2,1)}, u32[]{:S(2)}, u32[]{:S(2)}) async-start(bf16[16,64,256]{2,1,0:T(8,128)(2,1)} %broadcast_in_dim.25), calls=%async_computation.1 | async-start | bytes 1048576 | tf_op jit(solution)/shard_map/all_to_all | solution.py:50
  67.8 24.1 %collective-permute-start.2 = (bf16[1024,256]{1,0:T(8,128)(2,1)}, bf16[1024,256]{1,0:T(8,128)(2,1)}, u32[]{:S(2)}, u32[]{:S(2)}) collective-permute-start(bf16[1024,256]{1,0:T(8,128)(2,1)} %bitcast.107), channel_id=1, source_target_pairs={{0,32},{32,64},{64,96},{96,128},{128,160},{160,192},{192,224},{224... | collective-permute-start | bytes 1572872 | tf_op jit(solution)/shard_map/ppermute | solution.py:60
  93.2 19.2 %copy-start.1 = (bf16[1024,256]{1,0:T(8,128)(2,1)}, bf16[1024,256]{1,0:T(8,128)(2,1)S(1)}, u32[]{:S(2)}) copy-start(bf16[1024,256]{1,0:T(8,128)(2,1)S(1)} %bitcast_select_fusion.2) | copy-start | bytes 1572868
  93.2 13.8 %collective-permute-start.3 = (bf16[1024,256]{1,0:T(8,128)(2,1)S(1)}, bf16[1024,256]{1,0:T(8,128)(2,1)S(1)}, u32[]{:S(2)}, u32[]{:S(2)}) collective-permute-start(bf16[1024,256]{1,0:T(8,128)(2,1)S(1)} %bitcast_select_fusion.2), channel_id=1, source_target_pairs={{0,1},{1,2},{2,3},{3,4},{4,5},{5,6},{6,7},{7,8},{8,9},{9,10},{10,1... | collective-permute-start | bytes 1572872 | tf_op jit(solution)/shard_map/ppermute | solution.py:24
  98.5 13.6 %collective-permute-start.4 = (bf16[1024,256]{1,0:T(8,128)(2,1)S(1)}, bf16[1024,256]{1,0:T(8,128)(2,1)S(1)}, u32[]{:S(2)}, u32[]{:S(2)}) collective-permute-start(bf16[1024,256]{1,0:T(8,128)(2,1)S(1)} %bitcast_select_fusion.2), channel_id=1, source_target_pairs={{1,0},{2,1},{3,2},{4,3},{5,4},{6,5},{7,6},{8,7},{9,8},{10,9},{11,1... | collective-permute-start | bytes 1572872 | tf_op jit(solution)/shard_map/ppermute | solution.py:25
  149.7 29.0 %all-to-all-start.3 = ((bf16[16,64,256]{2,1,0:T(8,128)(2,1)}), bf16[16,64,256]{2,1,0:T(8,128)(2,1)}, u32[]{:S(2)}, u32[]{:S(2)}) async-start(bf16[16,64,256]{2,1,0:T(8,128)(2,1)} %broadcast_in_dim.26), calls=%async_computation.3 | async-start | bytes 1048576 | tf_op jit(solution)/shard_map/all_to_all | solution.py:50
  154.1 24.7 %collective-permute-start.5 = (bf16[1024,256]{1,0:T(8,128)(2,1)}, bf16[1024,256]{1,0:T(8,128)(2,1)}, u32[]{:S(2)}, u32[]{:S(2)}) collective-permute-start(bf16[1024,256]{1,0:T(8,128)(2,1)} %copy-done.1), channel_id=1, source_target_pairs={{0,32},{32,64},{64,96},{96,128},{128,160},{160,192},{192,224},{224... | collective-permute-start | bytes 1572872 | tf_op jit(solution)/shard_map/ppermute | solution.py:60
  180.0 18.9 %copy-start.2 = (bf16[1024,256]{1,0:T(8,128)(2,1)}, bf16[1024,256]{1,0:T(8,128)(2,1)S(1)}, u32[]{:S(2)}) copy-start(bf16[1024,256]{1,0:T(8,128)(2,1)S(1)} %bitcast_select_fusion.1) | copy-start | bytes 1572868
  180.0 13.7 %collective-permute-start.6 = (bf16[1024,256]{1,0:T(8,128)(2,1)S(1)}, bf16[1024,256]{1,0:T(8,128)(2,1)S(1)}, u32[]{:S(2)}, u32[]{:S(2)}) collective-permute-start(bf16[1024,256]{1,0:T(8,128)(2,1)S(1)} %bitcast_select_fusion.1), channel_id=1, source_target_pairs={{0,1},{1,2},{2,3},{3,4},{4,5},{5,6},{6,7},{7,8},{8,9},{9,10},{10,1... | collective-permute-start | bytes 1572872 | tf_op jit(solution)/shard_map/ppermute | solution.py:24
  185.2 13.6 %collective-permute-start.7 = (bf16[1024,256]{1,0:T(8,128)(2,1)S(1)}, bf16[1024,256]{1,0:T(8,128)(2,1)S(1)}, u32[]{:S(2)}, u32[]{:S(2)}) collective-permute-start(bf16[1024,256]{1,0:T(8,128)(2,1)S(1)} %bitcast_select_fusion.1), channel_id=1, source_target_pairs={{1,0},{2,1},{3,2},{4,3},{5,4},{6,5},{7,6},{8,7},{9,8},{10,9},{11,1... | collective-permute-start | bytes 1572872 | tf_op jit(solution)/shard_map/ppermute | solution.py:25
  235.7 30.0 %all-to-all-start.5 = ((bf16[16,64,256]{2,1,0:T(8,128)(2,1)}), bf16[16,64,256]{2,1,0:T(8,128)(2,1)}, u32[]{:S(2)}, u32[]{:S(2)}) async-start(bf16[16,64,256]{2,1,0:T(8,128)(2,1)} %broadcast_in_dim.27), calls=%async_computation.5 | async-start | bytes 1048576 | tf_op jit(solution)/shard_map/all_to_all | solution.py:50
  240.4 24.5 %collective-permute-start.8 = (bf16[1024,256]{1,0:T(8,128)(2,1)}, bf16[1024,256]{1,0:T(8,128)(2,1)}, u32[]{:S(2)}, u32[]{:S(2)}) collective-permute-start(bf16[1024,256]{1,0:T(8,128)(2,1)} %copy-done.2), channel_id=1, source_target_pairs={{0,32},{32,64},{64,96},{96,128},{128,160},{160,192},{192,224},{224... | collective-permute-start | bytes 1572872 | tf_op jit(solution)/shard_map/ppermute | solution.py:60
  267.0 13.6 %collective-permute-start.10 = (bf16[1024,256]{1,0:T(8,128)(2,1)S(1)}, bf16[1024,256]{1,0:T(8,128)(2,1)S(1)}, u32[]{:S(2)}, u32[]{:S(2)}) collective-permute-start(bf16[1024,256]{1,0:T(8,128)(2,1)S(1)} %bitcast_select_fusion), channel_id=1, source_target_pairs={{1,0},{2,1},{3,2},{4,3},{5,4},{6,5},{7,6},{8,7},{9,8},{10,9},{11,1... | collective-permute-start | bytes 1572872 | tf_op jit(solution)/shard_map/ppermute | solution.py:25
  268.9 15.2 %collective-permute-start.9 = (bf16[1024,256]{1,0:T(8,128)(2,1)S(1)}, bf16[1024,256]{1,0:T(8,128)(2,1)S(1)}, u32[]{:S(2)}, u32[]{:S(2)}) collective-permute-start(bf16[1024,256]{1,0:T(8,128)(2,1)S(1)} %bitcast_select_fusion), channel_id=1, source_target_pairs={{0,1},{1,2},{2,3},{3,4},{4,5},{5,6},{6,7},{7,8},{8,9},{9,10},{10,1... | collective-permute-start | bytes 1572872 | tf_op jit(solution)/shard_map/ppermute | solution.py:24
where the time goes:
time: 325 us; the launch traced here: 323 us
  waiting for transfers between devices  122 us (38%)
  blocking collectives  89.8 us (28%)
  starting transfers between devices  70 us (22%)
  other arithmetic  15.6 us (5%)
  local copies, waits for them, and re-layouts  14.1 us (4%)
  matrix products  8.02 us (2%)
  between operations  3.48 us (1%)
    all_to_all x3, blocking collectives, summed_on_arrival(): lax.all_to_all(blocks, axis, split_axis=0, concat_axis=0, tiled=True)  89.8 us
    ppermute x3, waiting for transfers between devices, passed_along(): return lax.ppermute(block, axis, route)  64 us
    ppermute x4, waiting for transfers between devices, padded(): before = lax.ppermute(last, axis, up)  22.8 us
    ppermute x4, starting transfers between devices, padded(): before = lax.ppermute(last, axis, up)  20.3 us
    all_to_all x1, waiting for transfers between devices, summed_on_arrival(): lax.all_to_all(blocks, axis, split_axis=0, concat_axis=0, tiled=True)  17.6 us
    ppermute x4, waiting for transfers between devices, padded(): after = lax.ppermute(leading, axis, down)  17.1 us
    all_to_all x1, starting transfers between devices, summed_on_arrival(): lax.all_to_all(blocks, axis, split_axis=0, concat_axis=0, tiled=True)  16.9 us
    all_to_all x3, starting transfers between devices, from_everyone(): return lax.all_to_all(copies, axis, split_axis=0, concat_axis=0, tiled=True)  15.9 us
  transfers between devices with their start and end apart: 15, of which 13 were waited for; matrix products, arithmetic and copies ran while one was open for 0% of the time, Pallas kernels for 0%

commit v1 on v0

v1 whole, which is shorter than its diff:
```python
import functools

import jax
import jax.numpy as jnp
from jax import lax
from jax.experimental import pallas as pl
from jax.experimental.pallas import tpu as pltpu
from jax.sharding import PartitionSpec as P

SHELL = 3
STEPS = 4
NEWTON = 3
MESH = pl.DeviceIdType.MESH

damping = 0.5
time_step = 0.25
creep_square = 0.01


def inverse_sinh(value):
    magnitude = jnp.abs(value)
    positive = jnp.log(magnitude + jnp.sqrt(magnitude * magnitude + 1.0))
    return jnp.where(value < 0.0, -positive, positive)


def settle_friction(shear_load, state_now, coef_a, coef_b, sigma):
    scale = 0.5 * jnp.exp(coef_b / coef_a * state_now)
    strength = sigma * coef_a
    velocity = shear_load / (strength * scale + damping)
    for iteration in range(NEWTON):
        scaled = scale * velocity
        residual = strength * inverse_sinh(scaled) + damping * velocity - shear_load
        derivative = strength * scale / jnp.sqrt(1.0 + scaled * scaled) + damping
        velocity = velocity - residual / derivative
    speed = jnp.sqrt(velocity * velocity + creep_square)
    new_state = state_now + time_step * (jnp.exp(-state_now) - speed)
    return velocity.astype(jnp.bfloat16), new_state


def kernel(
    n_lag,
    n_elem,
    k_hbm,
    shell_ref,
    cone_ref,
    h_hbm,
    stress_hbm,
    state_hbm,
    a_ref,
    b_ref,
    s_ref,
    rates_ref,
    final_ref,
    kbuf,
    win,
    stage,
    recv,
    vst,
    stress,
    state,
    weights,
    src,
    load_sem,
    sem_b,
    sem_l,
    sem_r,
    sem_rs,
    send_x,
    send_s,
    send_rs,
    send_v,
):
    lag = lax.axis_index("lag")
    elem = lax.axis_index("elem")
    own, depth = kbuf.shape
    block = depth // SHELL
    blocks = 3 * own // block
    rows = own // n_lag
    odd = elem % 2
    partner = elem + 1 - 2 * odd
    other = elem - 1 + 2 * odd
    has_other = (other >= 0) & (other < n_elem)
    has_left = elem > 0
    has_right = elem < n_elem - 1
    is_root = lag == 0
    left_part, mid_part, right_part = (pl.ds(i * own, own) for i in range(3))

    def dev(l, e):
        return {"lag": l, "elem": e}

    load_k = pltpu.make_async_copy(k_hbm.at[0], kbuf, load_sem.at[0])
    load_h = pltpu.make_async_copy(h_hbm.at[0], win.at[0, mid_part], load_sem.at[1])
    load_p = pltpu.make_async_copy(stress_hbm.at[0, 0], stress, load_sem.at[2])
    load_s = pltpu.make_async_copy(state_hbm.at[0, 0], state, load_sem.at[3])
    load_h.start()
    load_k.start()
    load_p.start()
    load_s.start()

    barrier = pltpu.get_barrier_semaphore()

    def greet(i, carry):
        pl.semaphore_signal(
            barrier, inc=1, device_id=dev((lag + 1 + i) % n_lag, elem), device_id_type=MESH
        )
        return carry

    lax.fori_loop(0, n_lag - 1, greet, 0)

    @pl.when(has_left)
    def _():
        pl.semaphore_signal(barrier, inc=1, device_id=dev(lag, elem - 1), device_id_type=MESH)

    @pl.when(has_right)
    def _():
        pl.semaphore_signal(barrier, inc=1, device_id=dev(lag, elem + 1), device_id_type=MESH)

    @pl.when(is_root & has_other)
    def _():
        def greet_other(i, carry):
            pl.semaphore_signal(barrier, inc=1, device_id=dev(1 + i, other), device_id_type=MESH)
            return carry

        lax.fori_loop(0, n_lag - 1, greet_other, 0)

    @pl.when(jnp.logical_not(has_left))
    def _():
        for t in range(STEPS):
            win[t, left_part] = jnp.zeros((own, win.shape[2]), win.dtype)

    @pl.when(jnp.logical_not(has_right))
    def _():
        for t in range(STEPS):
            win[t, right_part] = jnp.zeros((own, win.shape[2]), win.dtype)

    greeters = n_lag - 1 + jnp.where(has_left, 1, 0) + jnp.where(has_right, 1, 0)
    greeters = greeters + jnp.where(jnp.logical_not(is_root) & has_other, 1, 0)
    pl.semaphore_wait(barrier, greeters)

    def put(src, dst, send_sem, recv_sem, where):
        pltpu.make_async_remote_copy(
            src_ref=src,
            dst_ref=dst,
            send_sem=send_sem,
            recv_sem=recv_sem,
            device_id=where,
            device_id_type=MESH,
        ).start()

    def wait_for(ref, sem):
        pltpu.make_async_copy(ref, ref, sem).wait()

    def exchange(t):
        @pl.when(has_left)
        def _():
            put(win.at[t, mid_part], win.at[t, right_part], send_x.at[t], sem_r.at[t], dev(lag, elem - 1))

        @pl.when(has_right)
        def _():
            put(win.at[t, mid_part], win.at[t, left_part], send_x.at[t], sem_l.at[t], dev(lag, elem + 1))

    def to_partner(t):
        @pl.when(odd == 1)
        def _():
            put(win.at[t, mid_part], win.at[t, right_part], send_x.at[t], sem_r.at[t], dev(lag, partner))

        @pl.when(odd == 0)
        def _():
            put(win.at[t, mid_part], win.at[t, left_part], send_x.at[t], sem_l.at[t], dev(lag, partner))

    def shift(t):
        @pl.when(lag < n_lag - 1)
        def _():
            put(win.at[t, mid_part], win.at[t + 1, mid_part], send_s.at[t], sem_b.at[t + 1], dev(lag + 1, elem))

    def wait_sides(t):
        @pl.when(has_left)
        def _():
            wait_for(win.at[t, left_part], sem_l.at[t])

        @pl.when(has_right)
        def _():
            wait_for(win.at[t, right_part], sem_r.at[t])

    tile = min(256, own)
    per_tile = tile // rows

    picks = shell_ref[0]
    live = cone_ref[...]
    for k in range(SHELL):
        for j in range(blocks):
            chosen = (picks[:, k : k + 1] == j) & (live > k)
            weight = jnp.broadcast_to(jnp.where(chosen, 1.0, 0.0), weights.shape[1:])
            weights[k * blocks + j] = weight.astype(weights.dtype)

    def pick_sources(t):
        strip = weights.shape[1]

        def one_strip(i, carry):
            pieces = [
                win[t, pl.ds(pl.multiple_of(j * block + i * strip, strip), strip), :]
                for j in range(blocks)
            ]
            for k in range(SHELL):
                value = pieces[0] * weights[k * blocks]
                for j in range(1, blocks):
                    value = value + pieces[j] * weights[k * blocks + j]
                src[pl.ds(pl.multiple_of(k * block + i * strip, strip), strip), :] = value
            return carry

        lax.fori_loop(0, block // strip, one_strip, 0)

    def products(t):
        pick_sources(t)

        def one_tile(j, carry):
            total = jnp.dot(
                kbuf[pl.ds(pl.multiple_of(j * tile, tile), tile), :],
                src[...],
                preferred_element_type=jnp.float32,
            )
            stage[t, pl.ds(pl.multiple_of(j * tile, tile), tile), :] = total.astype(stage.dtype)
            for q in range(per_tile):
                peer = j * per_tile + q

                @pl.when(peer != lag)
                def _():
                    put(
                        stage.at[t, pl.ds(pl.multiple_of(peer * rows, rows), rows)],
                        recv.at[t, (peer - lag - 1 + n_lag) % n_lag],
                        send_rs.at[t],
                        sem_rs.at[t],
                        dev(peer, elem),
                    )

            return carry

        lax.fori_loop(0, own // tile, one_tile, 0)

    def column(ref):
        row = lax.broadcasted_iota(jnp.int32, (rows, rows), 0)
        col = lax.broadcasted_iota(jnp.int32, (rows, rows), 1)
        return jnp.sum(jnp.where(row == col, ref[0], 0.0), axis=1, keepdims=True)

    def settle(t):
        wait_for(recv.at[t], sem_rs.at[t])
        total = stage[t, pl.ds(pl.multiple_of(lag * rows, rows), rows), :].astype(jnp.float32)
        for i in range(n_lag - 1):
            total = total + recv[t, i].astype(jnp.float32)
        rates, new_state = settle_friction(
            stress[...] + total, state[...], column(a_ref), column(b_ref), column(s_ref)
        )
        if t < STEPS - 1:
            state[...] = new_state
            vst[t] = rates
            spot = pl.ds(pl.multiple_of(lag * rows, rows), rows)

            @pl.when(jnp.logical_not(is_root))
            def _():
                put(
                    vst.at[t],
                    win.at[t + 1, pl.ds(pl.multiple_of(own + lag * rows, rows), rows)],
                    send_v.at[t],
                    sem_b.at[t + 1],
                    dev(0, elem),
                )

            @pl.when(is_root)
            def _():
                win[t + 1, pl.ds(own, rows)] = rates

            @pl.when(has_other & (odd == 1))
            def _():
                put(vst.at[t], win.at[t + 1, spot], send_v.at[t], sem_l.at[t + 1], dev(0, other))

            @pl.when(has_other & (odd == 0))
            def _():
                put(
                    vst.at[t],
                    win.at[t + 1, pl.ds(pl.multiple_of(2 * own + lag * rows, rows), rows)],
                    send_v.at[t],
                    sem_r.at[t + 1],
                    dev(0, other),
                )
        else:
            rates_ref[0, 0] = rates
            final_ref[0, 0] = new_state

    load_h.wait()
    exchange(0)
    shift(0)
    load_k.wait()
    load_p.wait()
    load_s.wait()
    wait_sides(0)
    products(0)
    for t in range(STEPS):
        if t + 1 < STEPS:

            @pl.when(jnp.logical_not(is_root))
            def _():
                wait_for(win.at[t + 1, mid_part], sem_b.at[t + 1])
                exchange(t + 1)

        settle(t)
        if t + 1 < STEPS:

            @pl.when(is_root)
            def _():
                wait_for(win.at[t + 1, pl.ds(own + rows, own - rows)], sem_b.at[t + 1])
                to_partner(t + 1)

            if t + 2 < STEPS:
                shift(t + 1)
            wait_sides(t + 1)
            products(t + 1)

    for t in range(STEPS):
        wait_for(recv.at[t], send_rs.at[t])
        if t == 0:

            @pl.when(has_left)
            def _():
                wait_for(win.at[t, mid_part], send_x.at[t])

            @pl.when(has_right)
            def _():
                wait_for(win.at[t, mid_part], send_x.at[t])

        else:

            @pl.when(is_root)
            def _():
                wait_for(win.at[t, mid_part], send_x.at[t])

            @pl.when(jnp.logical_not(is_root) & has_left)
            def _():
                wait_for(win.at[t, mid_part], send_x.at[t])

            @pl.when(jnp.logical_not(is_root) & has_right)
            def _():
                wait_for(win.at[t, mid_part], send_x.at[t])

        if t + 1 < STEPS:

            @pl.when(lag < n_lag - 1)
            def _():
                wait_for(win.at[t, mid_part], send_s.at[t])

            @pl.when(jnp.logical_not(is_root))
            def _():
                wait_for(vst.at[t], send_v.at[t])

            @pl.when(has_other)
            def _():
                wait_for(vst.at[t], send_v.at[t])


def shards(n_lag, n_elem, kernel_tiles, shell_index, cone_blocks, history, prestress, log_state, fric_a, fric_b, normal_stress):
    own, depth = kernel_tiles.shape[1:]
    rows, scenarios = prestress.shape[2:]
    half = jnp.bfloat16
    anywhere = pl.BlockSpec(memory_space=pl.ANY)
    local = pl.BlockSpec(memory_space=pltpu.VMEM)
    dma = pltpu.SemaphoreType.DMA
    return pl.pallas_call(
        functools.partial(kernel, n_lag, n_elem),
        out_shape=(
            jax.ShapeDtypeStruct((1, 1, rows, scenarios), half),
            jax.ShapeDtypeStruct((1, 1, rows, scenarios), jnp.float32),
        ),
        in_specs=[anywhere, local, local, anywhere, anywhere, anywhere, local, local, local],
        out_specs=(local, local),
        scratch_shapes=[
            pltpu.VMEM((own, depth), half),
            pltpu.VMEM((STEPS, 3 * own, scenarios), half),
            pltpu.VMEM((STEPS, own, scenarios), half),
            pltpu.VMEM((STEPS, n_lag - 1, rows, scenarios), half),
            pltpu.VMEM((STEPS, rows, scenarios), half),
            pltpu.VMEM((rows, scenarios), jnp.float32),
            pltpu.VMEM((rows, scenarios), jnp.float32),
            pltpu.VMEM((SHELL * 3 * own * SHELL // depth, 16, scenarios), half),
            pltpu.VMEM((depth, scenarios), half),
            dma((4,)),
            dma((STEPS,)),
            dma((STEPS,)),
            dma((STEPS,)),
            dma((STEPS,)),
            dma((STEPS,)),
            dma((STEPS,)),
            dma((STEPS,)),
            dma((STEPS,)),
        ],
        compiler_params=pltpu.CompilerParams(
            collective_id=0, has_side_effects=True, vmem_limit_bytes=48 * 1024 * 1024
        ),
    )(kernel_tiles, shell_index, cone_blocks.reshape(1, 1), history, prestress, log_state, fric_a, fric_b, normal_stress)


def solution(mesh):
    in_specs = (
        P("lag", "elem", None),
        P("lag", "elem", None),
        P("lag"),
        P("lag", "elem", None),
        P("elem", "lag", None, None),
        P("elem", "lag", None, None),
        P("elem", "lag", None),
        P("elem", "lag", None),
        P("elem", "lag", None),
    )
    out_specs = (P("elem", "lag", None, None), P("elem", "lag", None, None))
    body = functools.partial(shards, mesh.shape["lag"], mesh.shape["elem"])
    return jax.shard_map(body, mesh=mesh, in_specs=in_specs, out_specs=out_specs, check_vma=False)
```

time: 325 us -> 149 us (0.46)
  the two profiles are of different devices: /device:TPU:47 before, /device:TPU:5 now
where the time goes in v1:
time: 149 us
  Pallas kernels  139 us (93%)
  local copies, waits for them, and re-layouts  8.47 us (6%)
    pallas_call x1, Pallas kernels, shards(): pl.pallas_call(functools.partial(kernel, n_lag, n_elem), out_shape=(jax.S...  139 us
    unnamed x18, local copies, waits for them, and re-layouts  8.47 us

profile of v1, /device:TPU:5, one launch (start us, length us, event | category | flops | bytes accessed | tf_op | source)
XLA Modules:
  0.0 149.1 jit_solution(10234240278333582904)
XLA Ops:
  1.3 0.0 copy-start
  1.3 1.9 %copy-done = bf16[1,1024,1536]{2,1,0:T(8,128)(2,1)S(1)} copy-done((bf16[1,1024,1536]{2,1,0:T(8,128)(2,1)S(1)}, bf16[1,1024,1536]{2,1,0:T(8,128)(2,1)}, u32[]{:S(2)}) %copy-start) | copy-done | bytes 3145752
  3.2 0.0 copy-start.1
  3.2 1.0 copy-done.1
  4.2 0.0 copy-start.2
  4.2 0.8 copy-done.2
  5.1 0.0 copy-start.3
  5.1 0.8 copy-done.3
  5.9 0.0 copy-start.4
  5.9 0.7 copy-done.4
  6.5 0.0 copy-start.5
  6.5 0.7 copy-done.5
  7.2 0.0 copy-start.6
  7.2 0.7 copy-done.6
  7.9 0.0 copy-start.7
  7.9 0.7 copy-done.7
  8.5 139.3 %shard_map.104 = (bf16[1,1,64,256]{3,2,1,0:T(8,128)(2,1)S(1)}, f32[1,1,64,256]{3,2,1,0:T(8,128)S(1)}) custom-call(bf16[1,1024,1536]{2,1,0:T(8,128)(2,1)S(1)} %copy-done, s32[1,1,3]{2,1,0:T(1,128)S(1)} %copy-done.4, s32[1,1]{1,0:T(1,128)} %bitcast.1.cone_ref, bf16[1,1024,256]{2,1,0:T(8,128)(2,1)S(1)} %copy-done.1, f32[1,1,64,256]{3,2,1,0:T(8,128)S(1)} %copy-done.2, ...), custom_call_target="tpu_custom_call" | custom-call | tf_op jit(solution)/shard_map/pallas_call | solution.py:366
  147.8 0.6 copy.14
  148.4 0.6 copy.15
Async XLA Ops:
  1.3 1.9 %copy-start = (bf16[1,1024,1536]{2,1,0:T(8,128)(2,1)S(1)}, bf16[1,1024,1536]{2,1,0:T(8,128)(2,1)}, u32[]{:S(2)}) copy-start(bf16[1,1024,1536]{2,1,0:T(8,128)(2,1)} %k_hbm.1) | copy-start | bytes 9437188
  3.2 1.0 copy-start.1
  4.2 0.8 copy-start.2
  5.1 0.8 copy-start.3
  5.9 0.7 copy-start.4
  6.5 0.7 copy-start.5
  7.2 0.7 copy-start.6
  7.9 0.7 copy-start.7
